TPU v7x, 256 devices: a whole 4x4x8 slice. The times are simulated.
256 devices in a mesh: seq: 64 (over z, x, y_hi), head: 4 (over y_lo, core).
Axes of the slice: x: 4, y: 4 (y_hi: 2, y_lo: 2; y = y_hi * 2 + y_lo), z: 8, core: 2. Of those that a mesh axis runs over, the one named last changes fastest.
Arguments:
- queries: bfloat16 [16384, 24, 128], P('seq', 'head'), may hold values from -6 to 6
- key_vectors: bfloat16 [16384, 24, 128], P('seq', 'head'), may hold values from -6 to 6
- values: bfloat16 [16384, 24, 128], P('seq', 'head'), may hold values from -6 to 6
- out_grad: bfloat16 [16384, 24, 128], P('seq', 'head'), may hold values from -6 to 6
- ssm_input: bfloat16 [16384, 48, 128], P('seq', 'head'), may hold values from -6 to 6
- ssm_out_grad: bfloat16 [16384, 48, 128], P('seq', 'head'), may hold values from -1.5 to 1.5
- step_sizes: float32 [16384, 48], P('seq', 'head'), may hold values from 0 to 2, as said below
- decay_rates: float32 [48], P('head'), may hold values from -1 to 0, as said below
- skip_gains: float32 [48], P('head'), may hold values from 0.5 to 1.5
- bc_rows: bfloat16 [16384, 128], P('seq'), may hold values from -0.75 to 0.75
- saved_states: float32 [64, 48, 64, 128], P('seq', 'head'), may hold values from -6 to 6
Outputs:
- query_grad: bfloat16 [16384, 24, 128], P('seq', 'head')
- key_grad: bfloat16 [16384, 24, 128], P('seq', 'head')
- value_grad: bfloat16 [16384, 24, 128], P('seq', 'head')
- grad_inputs: bfloat16 [16384, 48, 128], P('seq', 'head')
- grad_steps: float32 [16384, 48], P('seq', 'head')
- grad_bc: float32 [16384, 128], P(('seq', 'head'))
- grad_decay: float32 [48], P('head')
- grad_skip: float32 [48], P('head')
Inputs may be any that keep to these rules, and one draw needn't show every extreme that they name: `step_sizes`: positive. `decay_rates`: negative.
All inputs are finite; a program needn't handle non-finite values.
Results may differ from a plain program's by a relative error of at most 0.0095.
Values may be sent and summed in bfloat16 or wider, within the bound.
A program may use at most 192 MiB of HBM per device.

v0:
```python
import functools
import math

import jax
import jax.numpy as jnp
from jax import lax
from jax.experimental import pallas as pl
from jax.experimental.pallas import tpu as pltpu
from jax.sharding import Mesh
from jax.sharding import PartitionSpec as P

NSTATE = 64
SEQ = ("seq_0", "seq_1", "seq_2")
SEQ_HEAD = ("seq_0", "seq_1", "seq_2", "head")
AXES = ("seq_0", "seq_1", "seq_2", "head")
MESH = pl.DeviceIdType.MESH
HIGHEST = lax.Precision.HIGHEST
NEG = -1e30
UNIT = 256
HD = 128
SCALE = HD**-0.5
SCALE2 = SCALE * math.log2(math.e)
PLANE = 8
ZS = 8
XS = 4
PAIRS = ZS * XS
BF = jnp.bfloat16
F32 = jnp.float32


def dot(a, b, dims, precision=None):
    return lax.dot_general(a, b, (dims, ((), ())), precision=precision, preferred_element_type=F32)


def nn(a, b, precision=None):
    return dot(a, b, ((1,), (0,)), precision)


def nt(a, b):
    return dot(a, b, ((1,), (1,)))


def tn(a, b):
    return dot(a, b, ((0,), (0,)))


def kernel(
    k6, v6, q6, g6, xs, dy, st, rates, skips, b_in, c_in, s0,
    dq6, dk6, dv6, gx, gst, gbc, gtot,
    kv, qg, stat, og, tscr, dscr,
    lb, sb, lrow, rrow, skr, whr, cbt, wsum, gb_acc, gc_acc, g0, ec,
    car, plin, eplane, pplane, zt, zin, incout, inc,
    gbcl, gbin, tsrc, tpl, tz_src, tz,
    yin_s, yin_r, x1_s, x1_r, x2_s, x2_r, st_s, st_r, yo_s, yo_r,
    s1_s, s1_r, s2_s, s2_r, s3_s, s3_r, hb_s, hb_r, ta_s, ta_r, tb_s, tb_r,
):
    z, x, yh, hd = [lax.axis_index(a) for a in AXES]
    yl, core = hd // 2, hd % 2
    j = z * XS + x
    m = x * 2 + yh
    other = (1 - yl) * 2 + core
    heads = xs.shape[0]

    def at_pair(d):
        t = (j + d + PAIRS) % PAIRS
        return (t // XS, t % XS, yh, hd)

    def at_plane(mm):
        return (z, mm // 2, mm % 2, hd)

    def at_z(zz):
        return (zz, x, yh, hd)

    def at_head(hh):
        return (z, x, yh, hh)

    def at_y(k):
        return (z, x, k, other)

    def rcopy(src, dst, ss, rs, to):
        return pltpu.make_async_remote_copy(
            src_ref=src, dst_ref=dst, send_sem=ss, recv_sem=rs, device_id=to, device_id_type=MESH
        )

    peers = [at_y(0), at_y(1), at_pair(1), at_pair(-1), at_pair(2), at_pair(-2)]
    peers += [at_plane((m + o) % PLANE) for o in range(1, PLANE)]
    peers += [at_z((z + o) % ZS) for o in range(1, ZS)]
    peers += [at_head((hd + o) % 4) for o in range(1, 4)]
    barrier = pltpu.get_barrier_semaphore()
    for p in peers:
        pl.semaphore_signal(barrier, inc=1, device_id=p, device_id_type=MESH)
    pl.semaphore_wait(barrier, len(peers))

    sources = ((k6, v6), (q6, g6))
    lands = ((kv, 4), (qg, 0))

    def y_in(h, w, t, k, sender):
        buf, base = lands[w]
        return rcopy(
            sources[w][t].at[3 * k + h], buf.at[base + sender, h, t],
            yin_s.at[w, h, t, k], yin_r.at[w, h, t, sender], at_y(k),
        )

    def start_y_in(h):
        for w in range(2):
            for t in range(2):
                for k in range(2):
                    y_in(h, w, t, k, yh).start()

    def wait_y_in(h, w):
        for t in range(2):
            for k in range(2):
                y_in(h, w, t, k, k).wait_recv()

    def hop(n, w, h):
        if w == 0:
            src, dst, to = (kv.at[pl.ds(6 - 2 * n, 2), h], kv.at[pl.ds(4 - 2 * n, 2), h], at_pair(1))
        else:
            src, dst, to = (qg.at[pl.ds(2 * n - 2, 2), h], qg.at[pl.ds(2 * n, 2), h], at_pair(-1))
        ss, rs = ((x1_s, x1_r), (x2_s, x2_r))[n - 1]
        return rcopy(src, dst, ss.at[w, h], rs.at[w, h], to)

    def stat_copy(h, d):
        return rcopy(
            stat.at[pl.ds(0, 2), h], stat.at[pl.ds(2 * d, 2), h],
            st_s.at[d - 1, h], st_r.at[d - 1, h], at_pair(-d),
        )

    outs = (dq6, dk6, dv6)

    def y_out(n, h, i, sender):
        return rcopy(
            og.at[n, h, i], outs[n].at[3 * sender + h],
            yo_s.at[n, h, i], yo_r.at[n, h, sender], at_y(i),
        )

    def s1(o, to_m, from_m):
        return rcopy(
            car.at[:, pl.ds(pl.multiple_of(8 * to_m, 8), 8), :], plin.at[from_m],
            s1_s.at[o - 1], s1_r.at[o - 1], at_plane(to_m),
        )

    def s2(o, to_z, from_z):
        return rcopy(zt, zin.at[from_z], s2_s.at[o - 1], s2_r.at[o - 1], at_z(to_z))

    def s3(o, to_m, from_m):
        return rcopy(
            incout.at[to_m], inc.at[:, pl.ds(pl.multiple_of(8 * from_m, 8), 8), :],
            s3_s.at[o - 1], s3_r.at[o - 1], at_plane(to_m),
        )

    def hb(o, to_h, from_h):
        return rcopy(
            gbcl.at[pl.ds(pl.multiple_of(64 * to_h, 64), 64), :], gbin.at[from_h],
            hb_s.at[o - 1], hb_r.at[o - 1], at_head(to_h),
        )

    def ta(o, to_m, from_m):
        return rcopy(tsrc, tpl.at[from_m], ta_s.at[o - 1], ta_r.at[o - 1], at_plane(to_m))

    def tb(o, to_z, from_z):
        return rcopy(tz_src, tz.at[from_z], tb_s.at[o - 1], tb_r.at[o - 1], at_z(to_z))

    def start_all(make, mine, count):
        for o in range(1, count):
            make(o, (mine + o) % count, mine).start()

    def recv_all(make, mine, count):
        for o in range(1, count):
            make(o, mine, (mine + count - o) % count).wait_recv()

    def sent_all(make, mine, count):
        for o in range(1, count):
            make(o, (mine + o) % count, mine).wait_send()

    rowi = lax.broadcasted_iota(jnp.int32, (UNIT, UNIT), 0)
    coli = lax.broadcasted_iota(jnp.int32, (UNIT, UNIT), 1)

    start_y_in(0)
    start_y_in(1)
    start_y_in(2)
    steps = st[...]
    inclusive = (coli <= rowi).astype(F32)
    lcol = nn(inclusive, steps * rates[...], HIGHEST)
    lrow[...] = lcol.T
    decays = jnp.exp(lcol[UNIT - 1 : UNIT, :])
    for h in range(heads):
        lb[h] = jnp.broadcast_to(lcol[:, h : h + 1], (UNIT, HD))
        sb[h] = jnp.broadcast_to(steps[:, h : h + 1], (UNIT, HD))

    def summary(h, carry):
        scaled = (dy[h].astype(F32) * jnp.exp(lb[h])).astype(BF)
        car[h] = tn(c_in[...], scaled)
        return carry

    lax.fori_loop(0, heads, summary, 0)
    car[heads] = jnp.broadcast_to(decays, (NSTATE, HD))
    start_all(s1, m, PLANE)
    plin[m] = car[:, pl.ds(pl.multiple_of(8 * m, 8), 8), :]

    cbt[...] = nt(b_in[...], c_in[...])

    def send_own(h):
        for w in range(2):
            wait_y_in(h, w)
            hop(1, w, h).start()

    def send_next(h):
        for w in range(2):
            hop(1, w, h).wait_recv()
            hop(2, w, h).start()

    send_own(0)

    recv_all(s1, m, PLANE)
    acc = [jnp.zeros((8, HD), F32)] * heads
    prod = [jnp.ones((8, HD), F32)] * heads
    tile_prod = jnp.ones((8, HD), F32)
    for mm in reversed(range(PLANE)):
        tile = plin[mm, heads]
        tile_prod = tile_prod * tile
        for h in range(heads):
            eplane[mm, h] = acc[h]
            pplane[mm, h] = prod[h]
            decay = jnp.broadcast_to(tile[:, h : h + 1], (8, HD))
            acc[h] = plin[mm, h] + decay * acc[h]
            prod[h] = prod[h] * decay
    for h in range(heads):
        zt[h] = acc[h]
    zt[heads] = tile_prod
    start_all(s2, z, ZS)
    zin[z] = zt[...]

    send_own(1)
    send_next(0)

    recv_all(s2, z, ZS)
    acc = [jnp.zeros((8, HD), F32)] * heads
    for zz in reversed(range(1, ZS)):
        tile = zin[zz, heads]
        for h in range(heads):
            decay = jnp.broadcast_to(tile[:, h : h + 1], (8, HD))
            acc[h] = jnp.where(zz > z, zin[zz, h] + decay * acc[h], acc[h])
    for mm in range(PLANE):
        for h in range(heads):
            incout[mm, h] = eplane[mm, h] + pplane[mm, h] * acc[h]
    start_all(s3, m, PLANE)
    inc[:, pl.ds(pl.multiple_of(8 * m, 8), 8), :] = incout[m]

    send_own(2)
    send_next(1)

    recv_all(s3, m, PLANE)
    for ref in (rrow, skr, whr, wsum, gb_acc, gc_acc, g0, ec, tsrc):
        ref[...] = jnp.zeros_like(ref)
    lanes = lax.broadcasted_iota(jnp.int32, (UNIT, HD), 1)

    def wide(t):
        return jnp.concatenate([t, t], axis=1)

    def grads(h, carry):
        b_rows, c_rows = (b_in[...], c_in[...])
        lc, sc = (lb[h], sb[h])
        lr = lrow[pl.ds(h, 1), :]
        x_h, dy_h = (xs[h], dy[h])
        cb = cbt[...]
        decay = jnp.exp(jnp.where(coli >= rowi, lr - wide(lc), NEG))
        crossed = decay * nt(x_h, dy_h)
        weighted = crossed * wide(sc)
        wsum[...] += weighted
        rrow[pl.ds(h, 1), :] = jnp.sum(weighted * cb, axis=0, keepdims=True)
        paired = crossed * cb
        mixing = (decay * cb).astype(BF)
        tail = jnp.exp(lc[UNIT - 1 : UNIT, :] - lc)
        weights = jnp.exp(lc)
        inc_f, s0_f = (inc[h], s0[h])
        inc_h, s0_h = (inc_f.astype(BF), s0_f.astype(BF))
        dy_f = dy_h.astype(F32)
        driven_grad = nn(mixing, dy_h) + tail * nn(b_rows, inc_h)
        gx[h] = (sc * driven_grad + skips[h] * dy_f).astype(BF)
        late = nt(x_h, inc_h) * tail[:, :NSTATE]
        gb_acc[...] += sc[:, :NSTATE] * late
        early = nt(dy_h, s0_h) * weights[:, :NSTATE]
        gc_acc[...] += early
        own = jnp.sum(paired[:, :HD] + paired[:, HD:], axis=1, keepdims=True)
        own = own + jnp.sum(late * b_rows.astype(F32), axis=1, keepdims=True)
        first = jnp.sum(early * c_rows.astype(F32), axis=1, keepdims=True)
        here = lanes == h
        g0[...] += jnp.where(here, own, 0.0)
        ec[...] += jnp.where(here, first, 0.0)
        skr[pl.ds(h, 1), :] = jnp.sum(dy_f * x_h.astype(F32), axis=0, keepdims=True)
        whr[pl.ds(h, 1), :] = jnp.sum(inc_f * s0_f, axis=0, keepdims=True)
        return carry

    lax.fori_loop(0, heads, grads, 0)
    w_all = wsum[...]
    gb_all = gb_acc[...] + nn(w_all, c_in[...].astype(F32), HIGHEST)
    gc_all = gc_acc[...] + nn(w_all.T, b_in[...].astype(F32), HIGHEST)
    gbcl[...] = jnp.concatenate([gb_all, gc_all], axis=1)
    start_all(hb, hd, 4)
    gbin[hd] = gbcl[pl.ds(pl.multiple_of(64 * hd, 64), 64), :]
    steps = st[...]
    early_all = ec[...]
    change = steps * g0[...] - rrow[...].T - early_all
    strict = (coli < rowi).astype(F32)
    whole = decays * jnp.sum(whr[...].T, axis=0, keepdims=True)
    grad_log = nn(strict, change, HIGHEST) + (jnp.sum(early_all, axis=0, keepdims=True) + whole)
    gst[...] = g0[...] + rates[...] * grad_log
    tsrc[0:1, :] = jnp.sum(steps * grad_log, axis=0, keepdims=True)
    tsrc[1:2, :] = jnp.sum(skr[...].T, axis=0, keepdims=True)
    start_all(ta, m, PLANE)
    tpl[m] = tsrc[...]

    send_next(2)

    def window(h):
        def block(i, carry):
            q, g = (qg[i, h, 0], qg[i, h, 1])
            top = None
            for u in range(5):
                s = nt(kv[i + u, h, 0], q) * SCALE2
                if u == 0:
                    s = jnp.where(rowi > coli, s, NEG)
                if u == 4:
                    s = jnp.where(rowi <= coli, s, NEG)
                else:
                    s = s + jnp.where(2 * j + i + u >= 4, 0.0, NEG)
                tscr[u] = s
                best = jnp.max(s, axis=0, keepdims=True)
                top = best if top is None else jnp.maximum(top, best)
            total = jnp.zeros((1, UNIT), F32)
            delta = jnp.zeros((1, UNIT), F32)
            for u in range(5):
                e = jnp.exp2(tscr[u] - top)
                dp = nt(kv[i + u, h, 1], g)
                total = total + jnp.sum(e, axis=0, keepdims=True)
                delta = delta + jnp.sum(e * dp, axis=0, keepdims=True)
                tscr[u] = e
                dscr[u] = dp
            inverse = 1.0 / total
            delta = delta * inverse
            out = jnp.zeros((HD, UNIT), F32)
            for u in range(5):
                ds = (tscr[u] * (dscr[u] - delta)).astype(BF)
                out = out + tn(kv[i + u, h, 0], ds)
            og[0, h, i] = (out * (inverse * SCALE)).T.astype(BF)
            stat[i, h, 0:1, :] = top + jnp.log2(total)
            stat[i, h, 1:2, :] = delta
            return carry

        lax.fori_loop(0, 2, block, 0)

    def key_pass(h):
        def block(i, carry):
            k, v = (kv[4 + i, h, 0], kv[4 + i, h, 1])
            dk = jnp.zeros((UNIT, HD), F32)
            dv = jnp.zeros((UNIT, HD), F32)
            for u in range(5):
                q, g = (qg[i + u, h, 0], qg[i + u, h, 1])
                s = nt(k, q) * SCALE2 - stat[i + u, h, 0:1, :]
                if u == 0:
                    s = jnp.where(coli >= rowi, s, NEG)
                else:
                    s = s + jnp.where(2 * j + i + u < 2 * PAIRS, 0.0, NEG)
                if u == 4:
                    s = jnp.where(coli < rowi, s, NEG)
                p = jnp.exp2(s)
                dv = dv + nn(p.astype(BF), g)
                ds = (p * (nt(v, g) - stat[i + u, h, 1:2, :])).astype(BF)
                dk = dk + nn(ds, q)
            og[1, h, i] = (dk * SCALE).astype(BF)
            og[2, h, i] = dv.astype(BF)
            return carry

        lax.fori_loop(0, 2, block, 0)

    def windows(h):
        hop(2, 0, h).wait_recv()
        window(h)
        for d in (1, 2):
            stat_copy(h, d).start()
        for i in range(2):
            y_out(0, h, i, yh).start()

    def keys(h):
        hop(2, 1, h).wait_recv()
        for d in (1, 2):
            stat_copy(h, d).wait_recv()
        key_pass(h)
        for n in (1, 2):
            for i in range(2):
                y_out(n, h, i, yh).start()

    for h in range(3):
        for ref in (stat,):
            ref[0:2, h] = jnp.zeros((2, 8, UNIT), F32)
    windows(0)
    windows(1)
    keys(0)

    recv_all(ta, m, PLANE)
    plane_sum = tpl[0]
    for mm in range(1, PLANE):
        plane_sum = plane_sum + tpl[mm]
    tz_src[...] = plane_sum
    start_all(tb, z, ZS)
    tz[z] = plane_sum

    windows(2)
    keys(1)

    recv_all(hb, hd, 4)
    gbc[...] = ((gbin[0] + gbin[1]) + gbin[2]) + gbin[3]
    recv_all(tb, z, ZS)
    total = tz[0]
    for zz in range(1, ZS):
        total = total + tz[zz]
    gtot[...] = total

    keys(2)

    for h in range(3):
        for n in range(3):
            for i in range(2):
                y_out(n, h, i, i).wait_recv()
    for h in range(3):
        for w in range(2):
            for t in range(2):
                for k in range(2):
                    y_in(h, w, t, k, yh).wait_send()
            for n in (1, 2):
                hop(n, w, h).wait_send()
        for d in (1, 2):
            stat_copy(h, d).wait_send()
        for n in range(3):
            for i in range(2):
                y_out(n, h, i, yh).wait_send()
    sent_all(s1, m, PLANE)
    sent_all(s2, z, ZS)
    sent_all(s3, m, PLANE)
    sent_all(hb, hd, 4)
    sent_all(ta, m, PLANE)
    sent_all(tb, z, ZS)


def shards(
    queries, key_vectors, values, out_grad, ssm_input, ssm_out_grad,
    step_sizes, decay_rates, skip_gains, bc_rows, saved_states,
):
    heads = ssm_input.shape[1]
    by_head = [
        jnp.transpose(t, (1, 0, 2))
        for t in (key_vectors, values, queries, out_grad, ssm_input, ssm_out_grad)
    ]
    steps = jnp.pad(step_sizes, ((0, 0), (0, HD - heads)))
    rates = jnp.pad(decay_rates, (0, HD - heads))[None, :]
    vmem = pl.BlockSpec(memory_space=pltpu.VMEM)
    smem = pl.BlockSpec(memory_space=pltpu.SMEM)

    def shape(s, t=F32):
        return jax.ShapeDtypeStruct(s, t)

    def scratch(s, t=F32):
        return pltpu.VMEM(s, t)

    dma = pltpu.SemaphoreType.DMA
    wide = (heads, UNIT, HD)
    tile = (8, HD)
    out = pl.pallas_call(
        kernel,
        name="mixers",
        out_shape=[
            shape((6, UNIT, HD), BF), shape((6, UNIT, HD), BF), shape((6, UNIT, HD), BF),
            shape(wide, BF), shape((UNIT, HD)), shape((UNIT // 4, HD)), shape(tile),
        ],
        in_specs=[vmem] * 8 + [smem] + [vmem] * 3,
        out_specs=[vmem] * 7,
        scratch_shapes=[
            scratch((6, 3, 2, UNIT, HD), BF), scratch((6, 3, 2, UNIT, HD), BF),
            scratch((6, 3, 8, UNIT)), scratch((3, 3, 2, UNIT, HD), BF),
            scratch((5, UNIT, UNIT)), scratch((5, UNIT, UNIT)),
            scratch(wide), scratch(wide), scratch((HD, UNIT)), scratch((HD, UNIT)),
            scratch((HD, HD)), scratch((HD, HD)), scratch((UNIT, UNIT)), scratch((UNIT, UNIT)),
            scratch((UNIT, NSTATE)), scratch((UNIT, NSTATE)), scratch((UNIT, HD)), scratch((UNIT, HD)),
            scratch((heads + 1, NSTATE, HD)), scratch((PLANE, heads + 1, *tile)),
            scratch((PLANE, heads, *tile)), scratch((PLANE, heads, *tile)),
            scratch((heads + 1, *tile)), scratch((ZS, heads + 1, *tile)),
            scratch((PLANE, heads, *tile)), scratch((heads, NSTATE, HD)),
            scratch((UNIT, HD)), scratch((4, UNIT // 4, HD)),
            scratch(tile), scratch((PLANE, *tile)), scratch(tile), scratch((ZS, *tile)),
            dma((2, 3, 2, 2)), dma((2, 3, 2, 2)), dma((2, 3)), dma((2, 3)), dma((2, 3)), dma((2, 3)),
            dma((2, 3)), dma((2, 3)), dma((3, 3, 2)), dma((3, 3, 2)),
            dma((7,)), dma((7,)), dma((7,)), dma((7,)), dma((7,)), dma((7,)),
            dma((3,)), dma((3,)), dma((7,)), dma((7,)), dma((7,)), dma((7,)),
        ],
        compiler_params=pltpu.CompilerParams(
            collective_id=0, has_side_effects=True, vmem_limit_bytes=60 * 1024 * 1024
        ),
    )(
        *by_head, steps, rates, skip_gains, bc_rows[:, :NSTATE], bc_rows[:, NSTATE:], saved_states[0]
    )
    dq6, dk6, dv6, gx, gst, gbc, gtot = out
    return (
        jnp.transpose(dq6, (1, 0, 2)),
        jnp.transpose(dk6, (1, 0, 2)),
        jnp.transpose(dv6, (1, 0, 2)),
        jnp.transpose(gx, (1, 0, 2)),
        gst[:, :heads],
        gbc,
        gtot[0, :heads],
        gtot[1, :heads],
    )


def solution(mesh):
    torus = Mesh(mesh.devices.reshape(ZS, XS, 2, mesh.shape["head"]), AXES)
    token_head = P(SEQ, "head", None)
    in_specs = (token_head,) * 6 + (
        P(SEQ, "head"), P("head"), P("head"), P(SEQ, None), P(SEQ, "head", None, None),
    )
    out_specs = (token_head,) * 4 + (P(SEQ, "head"), P(SEQ_HEAD, None), P("head"), P("head"))
    return jax.shard_map(shards, mesh=torus, in_specs=in_specs, out_specs=out_specs, check_vma=False)
```

profile of v0, /device:TPU:6, one launch (start us, length us, event | category | flops | bytes accessed | tf_op | source)
XLA Modules:
  0.0 122.8 jit_solution(14119730721053344436)
XLA Ops:
  0.6 0.0 copy-start.5
  0.6 0.6 copy-done.5
  1.3 0.5 pad_bitcast_fusion.rates
  1.8 0.8 copy.19
  2.6 0.0 copy-start.3
  2.6 0.7 pad.8.st
  3.3 0.2 copy-done.3
  3.5 0.7 fusion
  4.2 110.9 %mixers.1 = (bf16[6,256,128]{2,1,0:T(8,128)(2,1)}, bf16[6,256,128]{2,1,0:T(8,128)(2,1)}, bf16[6,256,128]{2,1,0:T(8,128)(2,1)}, bf16[12,256,128]{2,1,0:T(8,128)(2...) custom-call(bf16[6,256,128]{2,1,0:T(8,128)(2,1)} %bitcast.21, bf16[6,256,128]{2,1,0:T(8,128)(2,1)} %bitcast.22, ...), custom_call_target="tpu_custom_call" | custom-call | tf_op jit(solution)/shard_map/mixers/pallas_call | solution.py:469
  115.1 1.3 %slice_bitcast_fusion = (f32[12]{0:T(128)}, f32[12]{0:T(128)}) fusion(f32[8,128]{1,0:T(8,128)} %get-tuple-element.21), kind=kLoop, calls=%fused_computation | loop fusion | bytes 192 | tf_op jit(solution)/shard_map/squeeze | solution.py:511
  116.4 1.6 %copy.20 = f32[256,12]{0,1:T(8,128)} copy(f32[256,12]{1,0:T(8,128)} %bitcast.29) | data formatting | bytes 24576
  118.0 0.0 copy-start.2
  118.0 0.0 copy-start.1
  118.0 1.8 %copy.26 = bf16[256,6,128]{2,0,1:T(8,128)(2,1)} copy(bf16[256,6,128]{2,0,1:T(8,128)(2,1)} %bitcast.28) | data formatting | bytes 786432
  119.8 0.0 copy-done.2
  119.8 0.0 copy-start
  119.8 0.7 copy.27
  120.6 0.0 copy-done.1
  120.6 0.7 copy.28
  121.3 0.0 copy-done
  121.3 0.0 copy-start.4
  121.3 0.9 copy.29
  122.2 0.0 copy-done.4
  122.2 0.6 copy.30
Async XLA Ops:
  0.6 0.7 copy-start.5
  2.6 0.8 copy-start.3
  118.0 1.8 %copy-start.2 = (bf16[6,256,128]{2,1,0:T(8,128)(2,1)S(1)}, bf16[6,256,128]{2,1,0:T(8,128)(2,1)}, u32[]{:S(2)}) copy-start(bf16[6,256,128]{2,1,0:T(8,128)(2,1)} %get-tuple-element.16) | copy-start | bytes 1179652
  118.0 2.6 %copy-start.1 = (bf16[6,256,128]{2,1,0:T(8,128)(2,1)S(1)}, bf16[6,256,128]{2,1,0:T(8,128)(2,1)}, u32[]{:S(2)}) copy-start(bf16[6,256,128]{2,1,0:T(8,128)(2,1)} %get-tuple-element.17) | copy-start | bytes 1179652
  119.8 1.5 %copy-start = (bf16[12,256,128]{2,1,0:T(8,128)(2,1)S(1)}, bf16[12,256,128]{2,1,0:T(8,128)(2,1)}, u32[]{:S(2)}) copy-start(bf16[12,256,128]{2,1,0:T(8,128)(2,1)} %get-tuple-element.18) | copy-start | bytes 2359300
  121.3 0.9 copy-start.4
where the time goes:
time: 123 us
  Pallas kernels  111 us (90%)
  local copies, waits for them, and re-layouts  11.2 us (9%)
    pallas_call x1, Pallas kernels, shards(): pl.pallas_call(kernel, name='mixers', out_shape=[shape((6, UNIT, HD), BF)...  111 us
    unnamed x19, local copies, waits for them, and re-layouts  8.07 us

commit v1 on v0

--- a/solution.py
+++ b/solution.py
@@ -45,11 +45,11 @@
 
 
 def kernel(
-    k6, v6, q6, g6, xs, dy, st, rates, skips, b_in, c_in, s0,
-    dq6, dk6, dv6, gx, gst, gbc, gtot,
+    k6, v6, q6, g6, xs, dy, st, rates, skips, bc, s0,
+    dq6, dk6, dv6, gx, gst, gbc, gdec, gskip,
     kv, qg, stat, og, tscr, dscr,
     lb, sb, lrow, rrow, skr, whr, cbt, wsum, gb_acc, gc_acc, g0, ec,
-    car, plin, eplane, pplane, zt, zin, incout, inc,
+    b_in, c_in, ldr, str_, car, plin, eplane, pplane, zt, zin, incout, inc,
     gbcl, gbin, tsrc, tpl, tz_src, tz,
     yin_s, yin_r, x1_s, x1_r, x2_s, x2_r, st_s, st_r, yo_s, yo_r,
     s1_s, s1_r, s2_s, s2_r, s3_s, s3_r, hb_s, hb_r, ta_s, ta_r, tb_s, tb_r,
@@ -136,7 +136,7 @@
 
     def s1(o, to_m, from_m):
         return rcopy(
-            car.at[:, pl.ds(pl.multiple_of(8 * to_m, 8), 8), :], plin.at[from_m],
+            car.at[to_m], plin.at[from_m],
             s1_s.at[o - 1], s1_r.at[o - 1], at_plane(to_m),
         )
 
@@ -145,7 +145,7 @@
 
     def s3(o, to_m, from_m):
         return rcopy(
-            incout.at[to_m], inc.at[:, pl.ds(pl.multiple_of(8 * from_m, 8), 8), :],
+            incout.at[to_m], inc.at[from_m],
             s3_s.at[o - 1], s3_r.at[o - 1], at_plane(to_m),
         )
 
@@ -177,26 +177,48 @@
     coli = lax.broadcasted_iota(jnp.int32, (UNIT, UNIT), 1)
 
     start_y_in(0)
-    start_y_in(1)
-    start_y_in(2)
-    steps = st[...]
-    inclusive = (coli <= rowi).astype(F32)
-    lcol = nn(inclusive, steps * rates[...], HIGHEST)
-    lrow[...] = lcol.T
+    b_in[...] = bc[:, :NSTATE]
+    c_in[...] = bc[:, NSTATE:]
+    ldr[...] = jnp.zeros_like(ldr)
+    str_[...] = jnp.zeros_like(str_)
+    str_[0:heads, :] = st[...]
+    for h in range(heads):
+        ldr[h : h + 1, :] = st[h : h + 1, :] * rates[h]
+    lrow[...] = nn(ldr[...], (rowi <= coli).astype(F32), HIGHEST)
+    lcol = lrow[...].T
+    steps = str_[...].T
     decays = jnp.exp(lcol[UNIT - 1 : UNIT, :])
+    sublane = lax.broadcasted_iota(jnp.int32, (8, HD), 0)
+
+    def as_terms(row):
+        high = row.astype(BF).astype(F32)
+        middle = (row - high).astype(BF).astype(F32)
+        low = row - high - middle
+        terms = jnp.where(sublane == 0, high, jnp.where(sublane == 1, middle, low))
+        return jnp.where(sublane < 3, terms, 0.0).astype(BF)
+
+    def from_terms(tile):
+        return jnp.sum(tile.astype(F32), axis=0, keepdims=True)
+
     for h in range(heads):
         lb[h] = jnp.broadcast_to(lcol[:, h : h + 1], (UNIT, HD))
         sb[h] = jnp.broadcast_to(steps[:, h : h + 1], (UNIT, HD))
 
     def summary(h, carry):
         scaled = (dy[h].astype(F32) * jnp.exp(lb[h])).astype(BF)
-        car[h] = tn(c_in[...], scaled)
+        part = tn(c_in[...], scaled)
+        for i in range(PLANE):
+            car[i, h] = part[8 * i : 8 * i + 8].astype(BF)
         return carry
 
     lax.fori_loop(0, heads, summary, 0)
-    car[heads] = jnp.broadcast_to(decays, (NSTATE, HD))
+    decay_terms = as_terms(decays)
+    for i in range(PLANE):
+        car[i, heads] = decay_terms
     start_all(s1, m, PLANE)
-    plin[m] = car[:, pl.ds(pl.multiple_of(8 * m, 8), 8), :]
+    start_y_in(1)
+    start_y_in(2)
+    plin[m] = car[m]
 
     cbt[...] = nt(b_in[...], c_in[...])
 
@@ -215,42 +237,40 @@
     recv_all(s1, m, PLANE)
     acc = [jnp.zeros((8, HD), F32)] * heads
     prod = [jnp.ones((8, HD), F32)] * heads
-    tile_prod = jnp.ones((8, HD), F32)
+    row_prod = jnp.ones((1, HD), F32)
     for mm in reversed(range(PLANE)):
-        tile = plin[mm, heads]
-        tile_prod = tile_prod * tile
+        row = from_terms(plin[mm, heads])
+        row_prod = row_prod * row
         for h in range(heads):
             eplane[mm, h] = acc[h]
             pplane[mm, h] = prod[h]
-            decay = jnp.broadcast_to(tile[:, h : h + 1], (8, HD))
-            acc[h] = plin[mm, h] + decay * acc[h]
+            decay = jnp.broadcast_to(row[:, h : h + 1], (8, HD))
+            acc[h] = plin[mm, h].astype(F32) + decay * acc[h]
             prod[h] = prod[h] * decay
     for h in range(heads):
-        zt[h] = acc[h]
-    zt[heads] = tile_prod
+        zt[h] = acc[h].astype(BF)
+    zt[heads] = as_terms(row_prod)
     start_all(s2, z, ZS)
     zin[z] = zt[...]
 
     send_own(1)
-    send_next(0)
-
     recv_all(s2, z, ZS)
     acc = [jnp.zeros((8, HD), F32)] * heads
     for zz in reversed(range(1, ZS)):
-        tile = zin[zz, heads]
+        row = from_terms(zin[zz, heads])
         for h in range(heads):
-            decay = jnp.broadcast_to(tile[:, h : h + 1], (8, HD))
-            acc[h] = jnp.where(zz > z, zin[zz, h] + decay * acc[h], acc[h])
+            decay = jnp.broadcast_to(row[:, h : h + 1], (8, HD))
+            acc[h] = jnp.where(zz > z, zin[zz, h].astype(F32) + decay * acc[h], acc[h])
     for mm in range(PLANE):
         for h in range(heads):
-            incout[mm, h] = eplane[mm, h] + pplane[mm, h] * acc[h]
+            incout[mm, h] = (eplane[mm, h] + pplane[mm, h] * acc[h]).astype(BF)
     start_all(s3, m, PLANE)
-    inc[:, pl.ds(pl.multiple_of(8 * m, 8), 8), :] = incout[m]
-
+    inc[m] = incout[m]
+
+    send_next(0)
     send_own(2)
     send_next(1)
 
-    recv_all(s3, m, PLANE)
     for ref in (rrow, skr, whr, wsum, gb_acc, gc_acc, g0, ec, tsrc):
         ref[...] = jnp.zeros_like(ref)
     lanes = lax.broadcasted_iota(jnp.int32, (UNIT, HD), 1)
@@ -273,7 +293,8 @@
         mixing = (decay * cb).astype(BF)
         tail = jnp.exp(lc[UNIT - 1 : UNIT, :] - lc)
         weights = jnp.exp(lc)
-        inc_f, s0_f = (inc[h], s0[h])
+        inc_f = jnp.concatenate([inc[i, h].astype(F32) for i in range(PLANE)], axis=0)
+        s0_f = s0[h]
         inc_h, s0_h = (inc_f.astype(BF), s0_f.astype(BF))
         dy_f = dy_h.astype(F32)
         driven_grad = nn(mixing, dy_h) + tail * nn(b_rows, inc_h)
@@ -291,27 +312,6 @@
         skr[pl.ds(h, 1), :] = jnp.sum(dy_f * x_h.astype(F32), axis=0, keepdims=True)
         whr[pl.ds(h, 1), :] = jnp.sum(inc_f * s0_f, axis=0, keepdims=True)
         return carry
-
-    lax.fori_loop(0, heads, grads, 0)
-    w_all = wsum[...]
-    gb_all = gb_acc[...] + nn(w_all, c_in[...].astype(F32), HIGHEST)
-    gc_all = gc_acc[...] + nn(w_all.T, b_in[...].astype(F32), HIGHEST)
-    gbcl[...] = jnp.concatenate([gb_all, gc_all], axis=1)
-    start_all(hb, hd, 4)
-    gbin[hd] = gbcl[pl.ds(pl.multiple_of(64 * hd, 64), 64), :]
-    steps = st[...]
-    early_all = ec[...]
-    change = steps * g0[...] - rrow[...].T - early_all
-    strict = (coli < rowi).astype(F32)
-    whole = decays * jnp.sum(whr[...].T, axis=0, keepdims=True)
-    grad_log = nn(strict, change, HIGHEST) + (jnp.sum(early_all, axis=0, keepdims=True) + whole)
-    gst[...] = g0[...] + rates[...] * grad_log
-    tsrc[0:1, :] = jnp.sum(steps * grad_log, axis=0, keepdims=True)
-    tsrc[1:2, :] = jnp.sum(skr[...].T, axis=0, keepdims=True)
-    start_all(ta, m, PLANE)
-    tpl[m] = tsrc[...]
-
-    send_next(2)
 
     def window(h):
         def block(i, carry):
@@ -392,9 +392,32 @@
                 y_out(n, h, i, yh).start()
 
     for h in range(3):
-        for ref in (stat,):
-            ref[0:2, h] = jnp.zeros((2, 8, UNIT), F32)
+        stat[0:2, h] = jnp.zeros((2, 8, UNIT), F32)
     windows(0)
+
+    recv_all(s3, m, PLANE)
+    lax.fori_loop(0, heads // 2, grads, 0)
+    send_next(2)
+    lax.fori_loop(heads // 2, heads, grads, 0)
+    w_all = wsum[...]
+    gb_all = gb_acc[...] + nn(w_all, c_in[...].astype(F32), HIGHEST)
+    gc_all = gc_acc[...] + nn(w_all.T, b_in[...].astype(F32), HIGHEST)
+    gbcl[...] = jnp.concatenate([gb_all, gc_all], axis=1)
+    start_all(hb, hd, 4)
+    gbin[hd] = gbcl[pl.ds(pl.multiple_of(64 * hd, 64), 64), :]
+    early_all = ec[...]
+    change = steps * g0[...] - rrow[...].T - early_all
+    strict = (coli < rowi).astype(F32)
+    whole = decays * jnp.sum(whr[...].T, axis=0, keepdims=True)
+    grad_log = nn(strict, change, HIGHEST) + (jnp.sum(early_all, axis=0, keepdims=True) + whole)
+    own_rows, log_rows = (g0[...].T, grad_log.T)
+    for h in range(heads):
+        gst[h : h + 1, :] = own_rows[h : h + 1, :] + rates[h] * log_rows[h : h + 1, :]
+    tsrc[0:1, :] = jnp.sum(steps * grad_log, axis=0, keepdims=True)
+    tsrc[1:2, :] = jnp.sum(skr[...].T, axis=0, keepdims=True)
+    start_all(ta, m, PLANE)
+    tpl[m] = tsrc[...]
+
     windows(1)
     keys(0)
 
@@ -406,8 +429,8 @@
     start_all(tb, z, ZS)
     tz[z] = plane_sum
 
+    keys(1)
     windows(2)
-    keys(1)
 
     recv_all(hb, hd, 4)
     gbc[...] = ((gbin[0] + gbin[1]) + gbin[2]) + gbin[3]
@@ -415,7 +438,8 @@
     total = tz[0]
     for zz in range(1, ZS):
         total = total + tz[zz]
-    gtot[...] = total
+    gdec[...] = total[0:1, :heads]
+    gskip[...] = total[1:2, :heads]
 
     keys(2)
 
@@ -443,6 +467,30 @@
     sent_all(tb, z, ZS)
 
 
+def finish_kernel(*refs):
+    count = len(refs) // 2
+    sems = refs[-1]
+    copies = [
+        pltpu.make_async_copy(refs[n], refs[count + n], sems.at[n]) for n in range(count)
+    ]
+    for copy in copies:
+        copy.start()
+    for copy in copies:
+        copy.wait()
+
+
+def finish(arrays):
+    count = len(arrays)
+    return pl.pallas_call(
+        finish_kernel,
+        name="finish",
+        out_shape=[jax.ShapeDtypeStruct(a.shape, a.dtype) for a in arrays],
+        in_specs=[pl.BlockSpec(memory_space=pltpu.VMEM)] * count,
+        out_specs=[pl.BlockSpec(memory_space=pl.ANY)] * count,
+        scratch_shapes=[pltpu.SemaphoreType.DMA((count,))],
+    )(*[pltpu.with_memory_space_constraint(a, pltpu.VMEM) for a in arrays])
+
+
 def shards(
     queries, key_vectors, values, out_grad, ssm_input, ssm_out_grad,
     step_sizes, decay_rates, skip_gains, bc_rows, saved_states,
@@ -452,13 +500,11 @@
         jnp.transpose(t, (1, 0, 2))
         for t in (key_vectors, values, queries, out_grad, ssm_input, ssm_out_grad)
     ]
-    steps = jnp.pad(step_sizes, ((0, 0), (0, HD - heads)))
-    rates = jnp.pad(decay_rates, (0, HD - heads))[None, :]
     vmem = pl.BlockSpec(memory_space=pltpu.VMEM)
     smem = pl.BlockSpec(memory_space=pltpu.SMEM)
 
-    def shape(s, t=F32):
-        return jax.ShapeDtypeStruct(s, t)
+    def kept(s, t=F32):
+        return pltpu.VMEM(s, t)
 
     def scratch(s, t=F32):
         return pltpu.VMEM(s, t)
@@ -470,11 +516,12 @@
         kernel,
         name="mixers",
         out_shape=[
-            shape((6, UNIT, HD), BF), shape((6, UNIT, HD), BF), shape((6, UNIT, HD), BF),
-            shape(wide, BF), shape((UNIT, HD)), shape((UNIT // 4, HD)), shape(tile),
+            kept((6, UNIT, HD), BF), kept((6, UNIT, HD), BF), kept((6, UNIT, HD), BF),
+            kept(wide, BF), kept((heads, UNIT)), kept((UNIT // 4, HD)),
+            kept((1, heads)), kept((1, heads)),
         ],
-        in_specs=[vmem] * 8 + [smem] + [vmem] * 3,
-        out_specs=[vmem] * 7,
+        in_specs=[vmem] * 7 + [smem] * 2 + [vmem] * 2,
+        out_specs=[vmem] * 8,
         scratch_shapes=[
             scratch((6, 3, 2, UNIT, HD), BF), scratch((6, 3, 2, UNIT, HD), BF),
             scratch((6, 3, 8, UNIT)), scratch((3, 3, 2, UNIT, HD), BF),
@@ -482,10 +529,11 @@
             scratch(wide), scratch(wide), scratch((HD, UNIT)), scratch((HD, UNIT)),
             scratch((HD, HD)), scratch((HD, HD)), scratch((UNIT, UNIT)), scratch((UNIT, UNIT)),
             scratch((UNIT, NSTATE)), scratch((UNIT, NSTATE)), scratch((UNIT, HD)), scratch((UNIT, HD)),
-            scratch((heads + 1, NSTATE, HD)), scratch((PLANE, heads + 1, *tile)),
+            scratch((UNIT, NSTATE), BF), scratch((UNIT, NSTATE), BF), scratch((HD, UNIT)), scratch((HD, UNIT)),
+            scratch((PLANE, heads + 1, *tile), BF), scratch((PLANE, heads + 1, *tile), BF),
             scratch((PLANE, heads, *tile)), scratch((PLANE, heads, *tile)),
-            scratch((heads + 1, *tile)), scratch((ZS, heads + 1, *tile)),
-            scratch((PLANE, heads, *tile)), scratch((heads, NSTATE, HD)),
+            scratch((heads + 1, *tile), BF), scratch((ZS, heads + 1, *tile), BF),
+            scratch((PLANE, heads, *tile), BF), scratch((PLANE, heads, *tile), BF),
             scratch((UNIT, HD)), scratch((4, UNIT // 4, HD)),
             scratch(tile), scratch((PLANE, *tile)), scratch(tile), scratch((ZS, *tile)),
             dma((2, 3, 2, 2)), dma((2, 3, 2, 2)), dma((2, 3)), dma((2, 3)), dma((2, 3)), dma((2, 3)),
@@ -497,18 +545,18 @@
             collective_id=0, has_side_effects=True, vmem_limit_bytes=60 * 1024 * 1024
         ),
     )(
-        *by_head, steps, rates, skip_gains, bc_rows[:, :NSTATE], bc_rows[:, NSTATE:], saved_states[0]
+        *by_head, step_sizes.T, decay_rates, skip_gains, bc_rows, saved_states[0]
     )
-    dq6, dk6, dv6, gx, gst, gbc, gtot = out
+    dq6, dk6, dv6, gx, gst, gbc, gdec, gskip = finish(out)
     return (
         jnp.transpose(dq6, (1, 0, 2)),
         jnp.transpose(dk6, (1, 0, 2)),
         jnp.transpose(dv6, (1, 0, 2)),
         jnp.transpose(gx, (1, 0, 2)),
-        gst[:, :heads],
+        gst.T,
         gbc,
-        gtot[0, :heads],
-        gtot[1, :heads],
+        gdec[0],
+        gskip[0],
     )
 
 

time: 123 us -> 90.9 us (0.74)
  the two profiles are of different devices: /device:TPU:6 before, /device:TPU:70 now
where the time goes in v1:
time: 90.9 us; the launch traced here: 90.8 us
  Pallas kernels  90.2 us (99%)
    pallas_call x1, Pallas kernels, shards(): pl.pallas_call(kernel, name='mixers', out_shape=[kept((6, UNIT, HD), BF),...  88.8 us

profile of v1, /device:TPU:70, one launch (start us, length us, event | category | flops | bytes accessed | tf_op | source)
XLA Modules:
  0.0 90.8 jit_solution(172224364991858881)
XLA Ops:
  0.6 88.8 %mixers.1 = (bf16[6,256,128]{2,1,0:T(8,128)(2,1)S(1)}, bf16[6,256,128]{2,1,0:T(8,128)(2,1)S(1)}, bf16[6,256,128]{2,1,0:T(8,128)(2,1)S(1)}, bf16[12,256,128]{2,1,...) custom-call(bf16[6,256,128]{2,1,0:T(8,128)(2,1)} %bitcast.17, ...), custom_call_target="tpu_custom_call" | custom-call | tf_op jit(solution)/shard_map/mixers/pallas_call | solution.py:515
  89.5 1.3 %finish.1 = (bf16[6,256,128]{2,1,0:T(8,128)(2,1)}, bf16[6,256,128]{2,1,0:T(8,128)(2,1)}, bf16[6,256,128]{2,1,0:T(8,128)(2,1)}, bf16[12,256,128]{2,1,0:T(8,128)(2...) custom-call(bf16[6,256,128]{2,1,0:T(8,128)(2,1)S(1)} %get-tuple-element.24.refs_0_, ...), custom_call_target="tpu_custom_call" | custom-call | tf_op jit(solution)/shard_map/finish/pallas_call | solution.py:484

commit v2 on v1

--- a/solution.py
+++ b/solution.py
@@ -45,11 +45,12 @@
 
 
 def kernel(
-    k6, v6, q6, g6, xs, dy, st, rates, skips, bc, s0,
+    k6_in, v6_in, q6_in, g6_in, xs_in, dy_in, st_in, rates, skips, bc_in, s0_in,
     dq6, dk6, dv6, gx, gst, gbc, gdec, gskip,
+    k6, v6, q6, g6, xs, dy, st, bc, s0, load_sem,
     kv, qg, stat, og, tscr, dscr,
     lb, sb, lrow, rrow, skr, whr, cbt, wsum, gb_acc, gc_acc, g0, ec,
-    b_in, c_in, ldr, str_, car, plin, eplane, pplane, zt, zin, incout, inc,
+    gdr, b_in, c_in, ldr, str_, car, plin, eplane, pplane, zt, zin, incout, inc,
     gbcl, gbin, tsrc, tpl, tz_src, tz,
     yin_s, yin_r, x1_s, x1_r, x2_s, x2_r, st_s, st_r, yo_s, yo_r,
     s1_s, s1_r, s2_s, s2_r, s3_s, s3_r, hb_s, hb_r, ta_s, ta_r, tb_s, tb_r,
@@ -59,7 +60,7 @@
     j = z * XS + x
     m = x * 2 + yh
     other = (1 - yl) * 2 + core
-    heads = xs.shape[0]
+    heads = xs_in.shape[0]
 
     def at_pair(d):
         t = (j + d + PAIRS) % PAIRS
@@ -86,6 +87,17 @@
     peers += [at_plane((m + o) % PLANE) for o in range(1, PLANE)]
     peers += [at_z((z + o) % ZS) for o in range(1, ZS)]
     peers += [at_head((hd + o) % 4) for o in range(1, 4)]
+    loads = [
+        pltpu.make_async_copy(src, dst, load_sem.at[n])
+        for n, (src, dst) in enumerate(
+            (
+                (k6_in, k6), (v6_in, v6), (q6_in, q6), (g6_in, g6), (st_in, st),
+                (bc_in, bc), (dy_in, dy), (xs_in, xs), (s0_in, s0),
+            )
+        )
+    ]
+    for load in loads:
+        load.start()
     barrier = pltpu.get_barrier_semaphore()
     for p in peers:
         pl.semaphore_signal(barrier, inc=1, device_id=p, device_id_type=MESH)
@@ -176,7 +188,11 @@
     rowi = lax.broadcasted_iota(jnp.int32, (UNIT, UNIT), 0)
     coli = lax.broadcasted_iota(jnp.int32, (UNIT, UNIT), 1)
 
+    for load in loads[:4]:
+        load.wait()
     start_y_in(0)
+    for load in loads[4:]:
+        load.wait()
     b_in[...] = bc[:, :NSTATE]
     c_in[...] = bc[:, NSTATE:]
     ldr[...] = jnp.zeros_like(ldr)
@@ -204,14 +220,18 @@
         lb[h] = jnp.broadcast_to(lcol[:, h : h + 1], (UNIT, HD))
         sb[h] = jnp.broadcast_to(steps[:, h : h + 1], (UNIT, HD))
 
-    def summary(h, carry):
+    def summary_of(h):
         scaled = (dy[h].astype(F32) * jnp.exp(lb[h])).astype(BF)
         part = tn(c_in[...], scaled)
         for i in range(PLANE):
             car[i, h] = part[8 * i : 8 * i + 8].astype(BF)
+
+    def summary(n, carry):
+        for i in range(3):
+            summary_of(3 * n + i)
         return carry
 
-    lax.fori_loop(0, heads, summary, 0)
+    lax.fori_loop(0, heads // 3, summary, 0)
     decay_terms = as_terms(decays)
     for i in range(PLANE):
         car[i, heads] = decay_terms
@@ -231,6 +251,55 @@
         for w in range(2):
             hop(1, w, h).wait_recv()
             hop(2, w, h).start()
+
+    for ref in (rrow, skr, whr, wsum, gb_acc, gc_acc, g0, ec, tsrc):
+        ref[...] = jnp.zeros_like(ref)
+    lanes = lax.broadcasted_iota(jnp.int32, (UNIT, HD), 1)
+
+    def wide(t):
+        return jnp.concatenate([t, t], axis=1)
+
+    def grads(h, carry):
+        c_rows = c_in[...]
+        lc, sc = (lb[h], sb[h])
+        lr = lrow[pl.ds(h, 1), :]
+        x_h, dy_h = (xs[h], dy[h])
+        cb = cbt[...]
+        decay = jnp.exp(jnp.where(coli >= rowi, lr - wide(lc), NEG))
+        crossed = decay * nt(x_h, dy_h)
+        weighted = crossed * wide(sc)
+        wsum[...] += weighted
+        rrow[pl.ds(h, 1), :] = jnp.sum(weighted * cb, axis=0, keepdims=True)
+        paired = crossed * cb
+        gdr[h] = nn((decay * cb).astype(BF), dy_h)
+        early = nt(dy_h, s0[h].astype(BF)) * jnp.exp(lc)[:, :NSTATE]
+        gc_acc[...] += early
+        own = jnp.sum(paired[:, :HD] + paired[:, HD:], axis=1, keepdims=True)
+        first = jnp.sum(early * c_rows.astype(F32), axis=1, keepdims=True)
+        here = lanes == h
+        g0[...] += jnp.where(here, own, 0.0)
+        ec[...] += jnp.where(here, first, 0.0)
+        skr[pl.ds(h, 1), :] = jnp.sum(dy_h.astype(F32) * x_h.astype(F32), axis=0, keepdims=True)
+        return carry
+
+    def carried_of(h):
+        b_rows = b_in[...]
+        lc, sc = (lb[h], sb[h])
+        tail = jnp.exp(lc[UNIT - 1 : UNIT, :] - lc)
+        inc_f = jnp.concatenate([inc[i, h].astype(F32) for i in range(PLANE)], axis=0)
+        inc_h = inc_f.astype(BF)
+        driven_grad = gdr[h] + tail * nn(b_rows, inc_h)
+        gx[h] = (sc * driven_grad + skips[h] * dy[h].astype(F32)).astype(BF)
+        late = nt(xs[h], inc_h) * tail[:, :NSTATE]
+        gb_acc[...] += sc[:, :NSTATE] * late
+        own = jnp.sum(late * b_rows.astype(F32), axis=1, keepdims=True)
+        g0[...] += jnp.where(lanes == h, own, 0.0)
+        whr[pl.ds(h, 1), :] = jnp.sum(inc_f * s0[h], axis=0, keepdims=True)
+
+    def carried(n, carry):
+        for i in range(2):
+            carried_of(2 * n + i)
+        return carry
 
     send_own(0)
 
@@ -254,6 +323,9 @@
     zin[z] = zt[...]
 
     send_own(1)
+    send_next(0)
+    send_own(2)
+    lax.fori_loop(0, heads // 2, grads, 0)
     recv_all(s2, z, ZS)
     acc = [jnp.zeros((8, HD), F32)] * heads
     for zz in reversed(range(1, ZS)):
@@ -267,51 +339,8 @@
     start_all(s3, m, PLANE)
     inc[m] = incout[m]
 
-    send_next(0)
-    send_own(2)
     send_next(1)
-
-    for ref in (rrow, skr, whr, wsum, gb_acc, gc_acc, g0, ec, tsrc):
-        ref[...] = jnp.zeros_like(ref)
-    lanes = lax.broadcasted_iota(jnp.int32, (UNIT, HD), 1)
-
-    def wide(t):
-        return jnp.concatenate([t, t], axis=1)
-
-    def grads(h, carry):
-        b_rows, c_rows = (b_in[...], c_in[...])
-        lc, sc = (lb[h], sb[h])
-        lr = lrow[pl.ds(h, 1), :]
-        x_h, dy_h = (xs[h], dy[h])
-        cb = cbt[...]
-        decay = jnp.exp(jnp.where(coli >= rowi, lr - wide(lc), NEG))
-        crossed = decay * nt(x_h, dy_h)
-        weighted = crossed * wide(sc)
-        wsum[...] += weighted
-        rrow[pl.ds(h, 1), :] = jnp.sum(weighted * cb, axis=0, keepdims=True)
-        paired = crossed * cb
-        mixing = (decay * cb).astype(BF)
-        tail = jnp.exp(lc[UNIT - 1 : UNIT, :] - lc)
-        weights = jnp.exp(lc)
-        inc_f = jnp.concatenate([inc[i, h].astype(F32) for i in range(PLANE)], axis=0)
-        s0_f = s0[h]
-        inc_h, s0_h = (inc_f.astype(BF), s0_f.astype(BF))
-        dy_f = dy_h.astype(F32)
-        driven_grad = nn(mixing, dy_h) + tail * nn(b_rows, inc_h)
-        gx[h] = (sc * driven_grad + skips[h] * dy_f).astype(BF)
-        late = nt(x_h, inc_h) * tail[:, :NSTATE]
-        gb_acc[...] += sc[:, :NSTATE] * late
-        early = nt(dy_h, s0_h) * weights[:, :NSTATE]
-        gc_acc[...] += early
-        own = jnp.sum(paired[:, :HD] + paired[:, HD:], axis=1, keepdims=True)
-        own = own + jnp.sum(late * b_rows.astype(F32), axis=1, keepdims=True)
-        first = jnp.sum(early * c_rows.astype(F32), axis=1, keepdims=True)
-        here = lanes == h
-        g0[...] += jnp.where(here, own, 0.0)
-        ec[...] += jnp.where(here, first, 0.0)
-        skr[pl.ds(h, 1), :] = jnp.sum(dy_f * x_h.astype(F32), axis=0, keepdims=True)
-        whr[pl.ds(h, 1), :] = jnp.sum(inc_f * s0_f, axis=0, keepdims=True)
-        return carry
+    lax.fori_loop(heads // 2, heads, grads, 0)
 
     def window(h):
         def block(i, carry):
@@ -394,11 +423,14 @@
     for h in range(3):
         stat[0:2, h] = jnp.zeros((2, 8, UNIT), F32)
     windows(0)
+    send_next(2)
+    windows(1)
+    keys(0)
+    windows(2)
+    keys(1)
 
     recv_all(s3, m, PLANE)
-    lax.fori_loop(0, heads // 2, grads, 0)
-    send_next(2)
-    lax.fori_loop(heads // 2, heads, grads, 0)
+    lax.fori_loop(0, heads // 2, carried, 0)
     w_all = wsum[...]
     gb_all = gb_acc[...] + nn(w_all, c_in[...].astype(F32), HIGHEST)
     gc_all = gc_acc[...] + nn(w_all.T, b_in[...].astype(F32), HIGHEST)
@@ -418,8 +450,7 @@
     start_all(ta, m, PLANE)
     tpl[m] = tsrc[...]
 
-    windows(1)
-    keys(0)
+    keys(2)
 
     recv_all(ta, m, PLANE)
     plane_sum = tpl[0]
@@ -428,10 +459,6 @@
     tz_src[...] = plane_sum
     start_all(tb, z, ZS)
     tz[z] = plane_sum
-
-    keys(1)
-    windows(2)
-
     recv_all(hb, hd, 4)
     gbc[...] = ((gbin[0] + gbin[1]) + gbin[2]) + gbin[3]
     recv_all(tb, z, ZS)
@@ -440,8 +467,6 @@
         total = total + tz[zz]
     gdec[...] = total[0:1, :heads]
     gskip[...] = total[1:2, :heads]
-
-    keys(2)
 
     for h in range(3):
         for n in range(3):
@@ -501,6 +526,7 @@
         for t in (key_vectors, values, queries, out_grad, ssm_input, ssm_out_grad)
     ]
     vmem = pl.BlockSpec(memory_space=pltpu.VMEM)
+    hbm = pl.BlockSpec(memory_space=pl.ANY)
     smem = pl.BlockSpec(memory_space=pltpu.SMEM)
 
     def kept(s, t=F32):
@@ -520,16 +546,20 @@
             kept(wide, BF), kept((heads, UNIT)), kept((UNIT // 4, HD)),
             kept((1, heads)), kept((1, heads)),
         ],
-        in_specs=[vmem] * 7 + [smem] * 2 + [vmem] * 2,
+        in_specs=[hbm] * 7 + [smem] * 2 + [hbm] * 2,
         out_specs=[vmem] * 8,
         scratch_shapes=[
+            scratch((6, UNIT, HD), BF), scratch((6, UNIT, HD), BF),
+            scratch((6, UNIT, HD), BF), scratch((6, UNIT, HD), BF),
+            scratch(wide, BF), scratch(wide, BF), scratch((heads, UNIT)),
+            scratch((UNIT, HD), BF), scratch((heads, NSTATE, HD)), dma((9,)),
             scratch((6, 3, 2, UNIT, HD), BF), scratch((6, 3, 2, UNIT, HD), BF),
             scratch((6, 3, 8, UNIT)), scratch((3, 3, 2, UNIT, HD), BF),
             scratch((5, UNIT, UNIT)), scratch((5, UNIT, UNIT)),
             scratch(wide), scratch(wide), scratch((HD, UNIT)), scratch((HD, UNIT)),
             scratch((HD, HD)), scratch((HD, HD)), scratch((UNIT, UNIT)), scratch((UNIT, UNIT)),
             scratch((UNIT, NSTATE)), scratch((UNIT, NSTATE)), scratch((UNIT, HD)), scratch((UNIT, HD)),
-            scratch((UNIT, NSTATE), BF), scratch((UNIT, NSTATE), BF), scratch((HD, UNIT)), scratch((HD, UNIT)),
+            scratch(wide), scratch((UNIT, NSTATE), BF), scratch((UNIT, NSTATE), BF), scratch((HD, UNIT)), scratch((HD, UNIT)),
             scratch((PLANE, heads + 1, *tile), BF), scratch((PLANE, heads + 1, *tile), BF),
             scratch((PLANE, heads, *tile)), scratch((PLANE, heads, *tile)),
             scratch((heads + 1, *tile), BF), scratch((ZS, heads + 1, *tile), BF),

time: 90.9 us -> 83.6 us (0.920)
  the two profiles are of different devices: /device:TPU:70 before, /device:TPU:8 now
where the time goes in v2:
time: 83.6 us; the launch traced here: 83.5 us
  Pallas kernels  82.9 us (99%)
    pallas_call x1, Pallas kernels, shards(): pl.pallas_call(kernel, name='mixers', out_shape=[kept((6, UNIT, HD), BF),...  81.5 us

profile of v2, /device:TPU:8, one launch (start us, length us, event | category | flops | bytes accessed | tf_op | source)
XLA Modules:
  0.0 83.5 jit_solution(7425050802804664930)
XLA Ops:
  0.6 81.5 %mixers.1 = (bf16[6,256,128]{2,1,0:T(8,128)(2,1)S(1)}, bf16[6,256,128]{2,1,0:T(8,128)(2,1)S(1)}, bf16[6,256,128]{2,1,0:T(8,128)(2,1)S(1)}, bf16[12,256,128]{2,1,...) custom-call(bf16[6,256,128]{2,1,0:T(8,128)(2,1)} %bitcast.17, ...), custom_call_target="tpu_custom_call" | custom-call | tf_op jit(solution)/shard_map/mixers/pallas_call | solution.py:541
  82.2 1.3 %finish.1 = (bf16[6,256,128]{2,1,0:T(8,128)(2,1)}, bf16[6,256,128]{2,1,0:T(8,128)(2,1)}, bf16[6,256,128]{2,1,0:T(8,128)(2,1)}, bf16[12,256,128]{2,1,0:T(8,128)(2...) custom-call(bf16[6,256,128]{2,1,0:T(8,128)(2,1)S(1)} %get-tuple-element.24.refs_0_, ...), custom_call_target="tpu_custom_call" | custom-call | tf_op jit(solution)/shard_map/finish/pallas_call | solution.py:509

commit v3 on v2

--- a/solution.py
+++ b/solution.py
@@ -174,7 +174,7 @@
         return rcopy(tz_src, tz.at[from_z], tb_s.at[o - 1], tb_r.at[o - 1], at_z(to_z))
 
     def start_all(make, mine, count):
-        for o in range(1, count):
+        for o in {4: (3, 1, 2), 8: (5, 3, 4, 7, 1, 6, 2) if mine is m else (4, 3, 5, 2, 6, 1, 7)}[count]:
             make(o, (mine + o) % count, mine).start()
 
     def recv_all(make, mine, count):
@@ -406,7 +406,7 @@
     def windows(h):
         hop(2, 0, h).wait_recv()
         window(h)
-        for d in (1, 2):
+        for d in (2, 1):
             stat_copy(h, d).start()
         for i in range(2):
             y_out(0, h, i, yh).start()
@@ -427,7 +427,6 @@
     windows(1)
     keys(0)
     windows(2)
-    keys(1)
 
     recv_all(s3, m, PLANE)
     lax.fori_loop(0, heads // 2, carried, 0)
@@ -449,6 +448,8 @@
     tsrc[1:2, :] = jnp.sum(skr[...].T, axis=0, keepdims=True)
     start_all(ta, m, PLANE)
     tpl[m] = tsrc[...]
+
+    keys(1)
 
     keys(2)
 

time: 83.6 us -> 80.8 us (0.967)
  the two profiles are of different devices: /device:TPU:8 before, /device:TPU:6 now
where the time goes in v3:
time: 80.8 us; the launch traced here: 80.4 us
  Pallas kernels  79.7 us (99%)
    pallas_call x1, Pallas kernels, shards(): pl.pallas_call(kernel, name='mixers', out_shape=[kept((6, UNIT, HD), BF),...  78.4 us

profile of v3, /device:TPU:6, one launch (start us, length us, event | category | flops | bytes accessed | tf_op | source)
XLA Modules:
  0.0 80.4 jit_solution(627969887958248392)
XLA Ops:
  0.6 78.4 %mixers.1 = (bf16[6,256,128]{2,1,0:T(8,128)(2,1)S(1)}, bf16[6,256,128]{2,1,0:T(8,128)(2,1)S(1)}, bf16[6,256,128]{2,1,0:T(8,128)(2,1)S(1)}, bf16[12,256,128]{2,1,...) custom-call(bf16[6,256,128]{2,1,0:T(8,128)(2,1)} %bitcast.17, ...), custom_call_target="tpu_custom_call" | custom-call | tf_op jit(solution)/shard_map/mixers/pallas_call | solution.py:542
  79.0 1.3 %finish.1 = (bf16[6,256,128]{2,1,0:T(8,128)(2,1)}, bf16[6,256,128]{2,1,0:T(8,128)(2,1)}, bf16[6,256,128]{2,1,0:T(8,128)(2,1)}, bf16[12,256,128]{2,1,0:T(8,128)(2...) custom-call(bf16[6,256,128]{2,1,0:T(8,128)(2,1)S(1)} %get-tuple-element.24.refs_0_, ...), custom_call_target="tpu_custom_call" | custom-call | tf_op jit(solution)/shard_map/finish/pallas_call | solution.py:510
